TPU v7x, 32 devices: a whole 2x2x4 slice. The times are simulated.
32 devices in a mesh: rep: 2 (over y), tp: 4 (over z), ep: 4 (over x, core).
Axes of the slice: x: 2, y: 2, z: 4, core: 2. Of those that a mesh axis runs over, the one named last changes fastest.
Arguments:
- tokens: bfloat16 [768, 3072], P(('rep', 'ep'), 'tp'), parts along dimension 0, may hold values from -6 to 6
- routing: int32 [768, 2], P(('rep', 'ep')), parts along dimension 0, may hold values from 0 to 3, all different within a row; in each aligned block of 96 rows (0 to 95, 96 to 191, ...) at most 54 rows name the same one
- route_gates: float32 [768, 2], P(('rep', 'ep')), parts along dimension 0, may hold values from 0.2 to 1
- expert_gate: bfloat16 [4, 3072, 8192], P('ep', None, 'tp'), may hold values from -0.109375 to 0.109375
- expert_up: bfloat16 [4, 3072, 8192], P('ep', None, 'tp'), may hold values from -0.109375 to 0.109375
- expert_down: bfloat16 [4, 8192, 3072], P('ep', 'tp'), may hold values from -0.0625 to 0.0625
Outputs:
- mixture: bfloat16 [768, 3072], P(('rep', 'ep'), 'tp'), parts along dimension 0
There are 2 independent parts, one for each index of `rep`. A program takes and returns all parts, laid end to end along the dimension named above; an argument that names none is the same for every part. Nothing has to cross between parts.
Inputs may be any that keep to these rules, and one draw needn't show every extreme that they name: `routing`: each token names two different experts. In each aligned block of 96 tokens (the rows of one index of ep) no expert is named by more than 54 tokens, a bound that some block reaches.
All inputs are finite; a program needn't handle non-finite values.
Results may differ from a plain program's by a relative error of at most 0.0085.
Values may be sent and summed in bfloat16 or wider, within the bound.
A program may use at most 128 MiB of HBM per device.

v0:
```python
import jax
import jax.numpy as jnp
from jax import lax
from jax.sharding import PartitionSpec as P


def slot_tables(routing, route_gates, experts, capacity):
    count_rows = routing.shape[0]
    choices_n = routing.shape[1]
    flat_ids = routing.reshape(-1)
    onehot = (flat_ids[:, None] == jnp.arange(experts, dtype=jnp.int32)[None, :]).astype(jnp.int32)
    before = jnp.cumsum(onehot, axis=0) - onehot
    position = jnp.sum(before * onehot, axis=1)
    slot_index = flat_ids * capacity + position
    picked = (
        slot_index[:, None] == jnp.arange(experts * capacity, dtype=jnp.int32)[None, :]
    ).astype(jnp.float32)
    dispatch = picked.reshape(count_rows, choices_n, experts * capacity).sum(axis=1)
    combine = (
        (picked * route_gates.reshape(-1)[:, None])
        .reshape(count_rows, choices_n, experts * capacity)
        .sum(axis=1)
    )
    return (dispatch, combine)


def hidden_rows(everyone, expert_gate, expert_up, capacity):
    local_count = expert_gate.shape[0]
    total = everyone.shape[0]
    row_block = everyone.reshape(
        total // (local_count * capacity), local_count, capacity, everyone.shape[1]
    )
    gate_part = jnp.einsum(
        "tlcd,ldf->tlcf", row_block, expert_gate, preferred_element_type=jnp.float32
    )
    upward = jnp.einsum("tlcd,ldf->tlcf", row_block, expert_up, preferred_element_type=jnp.float32)
    return (jax.nn.silu(gate_part) * upward).astype(jnp.bfloat16)


def body(tokens, routing, route_gates, expert_gate, expert_up, expert_down):
    local_count = expert_gate.shape[0]
    ep_count = lax.axis_size("ep")
    tp_count = lax.axis_size("tp")
    tok_count = tokens.shape[0]
    capacity = 2 * tok_count // ep_count + tok_count // 16
    experts = local_count * ep_count
    dispatch, combine = slot_tables(routing, route_gates, experts, capacity)
    dispatch_low = dispatch.astype(jnp.bfloat16)
    whole = lax.all_gather(tokens, "tp", axis=1, tiled=True)
    packed = jnp.einsum(
        "tc,td->cd", dispatch_low, whole, preferred_element_type=jnp.float32
    ).astype(jnp.bfloat16)
    everyone = lax.all_to_all(packed, "ep", split_axis=0, concat_axis=0, tiled=True)
    total_rows = everyone.shape[0]
    columns = everyone.shape[1]
    hidden = hidden_rows(everyone, expert_gate, expert_up, capacity)
    part = jnp.einsum("tlcf,lfd->dtlc", hidden, expert_down, preferred_element_type=jnp.float32)
    summed_t = lax.psum_scatter(
        part.reshape(columns // tp_count * lax.axis_size("tp"), total_rows),
        "tp",
        scatter_dimension=0,
        tiled=True,
    )
    summed = summed_t.T
    expert_out = summed.astype(jnp.bfloat16)
    returned = lax.all_to_all(expert_out, "ep", split_axis=0, concat_axis=0, tiled=True)
    mixed = jnp.dot(combine, returned.astype(jnp.float32), precision=lax.Precision.HIGHEST)
    return mixed.astype(jnp.bfloat16)


def solution(mesh):
    return jax.shard_map(
        body,
        mesh=mesh,
        in_specs=(
            P(("rep", "ep"), "tp"),
            P(("rep", "ep"), None),
            P(("rep", "ep"), None),
            P("ep", None, "tp"),
            P("ep", None, "tp"),
            P("ep", "tp", None),
        ),
        out_specs=P(("rep", "ep"), "tp"),
        check_vma=False,
    )
```

profile of v0, /device:TPU:0, one launch (start us, length us, event | category | flops | bytes accessed | tf_op | source)
XLA Modules:
  0.0 145.9 jit_solution(12279673939200975978)
XLA Ops:
  6.5 0.8 copy.23
  7.3 0.1 eq.37
  7.5 1.2 reduce-window.6
  8.7 0.1 slice.12
  8.8 0.1 copy.24
  8.9 0.1 copy.25
  9.0 0.1 add_bitcast_fusion
  9.1 0.1 reduce_sum.30
  9.3 0.7 multiply_add_fusion
  10.1 18.5 %all_gather.3 = bf16[96,3072]{1,0:T(8,128)(2,1)S(1)} all-gather(bf16[96,768]{1,0:T(8,128)(2,1)} %param.6), channel_id=1, replica_groups=mesh['rep'=2,'tp'=4,'ep'=4] {'tp'}, dimensions={1}, use_global_device_ids=true | all-gather | bytes 737280 | tf_op jit(solution)/shard_map/all_gather | solution.py:49
  28.5 0.8 convert_reduce_fusion
  29.3 0.5 convolution_convert_fusion
  29.9 0.4 all_to_all.14
  30.2 20.5 %all_to_all.21 = bf16[4,54,3072]{2,1,0:T(8,128)(2,1)S(1)} all-to-all(bf16[4,54,3072]{2,1,0:T(8,128)(2,1)S(1)} %all_to_all.14), channel_id=1, replica_groups=mesh['rep'=2,'tp'=4,'ep'=4] {'ep'}, dimensions={0} | all-to-all | bytes 2654208 | tf_op jit(solution)/shard_map/all_to_all | solution.py:53
  50.7 6.3 %fusion.9 = f32[4,1,54,2048]{3,2,0,1:T(8,128)S(1)} fusion(bf16[4,54,3072]{2,1,0:T(8,128)(2,1)S(1)} %all_to_all.21, bf16[1,3072,2048]{2,1,0:T(8,128)(2,1)} %param.9), kind=kOutput, calls=%fused_computation.8 | convolution fusion | flops 2717908992 | bytes 15679488 | tf_op jit(solution)/shard_map/tlcd,ldf->tlcf/dot_general | solution.py:33
  57.0 7.9 %fusion.18 = bf16[4,1,54,2048]{3,2,0,1:T(8,128)(2,1)S(1)} fusion(bf16[4,54,3072]{2,1,0:T(8,128)(2,1)S(1)} %all_to_all.21, bf16[1,3072,2048]{2,1,0:T(8,128)(2,1)} %param.10, f32[4,1,54,2048]{3,2,0,1:T(8,128)S(1)} %fusion.9), kind=kOutput, calls=%fused_computation.11 | convolution fusion | flops 2720563200 | bytes 16564224 | tf_op jit(solution)/shard_map/tlcd,ldf->tlcf/dot_general | solution.py:36
  64.9 0.2 dot_general.34
  65.1 9.0 %fusion.6 = f32[3072,216]{0,1:T(8,128)} fusion(bf16[216,2048]{1,0:T(8,128)(2,1)S(1)} %dot_general.34, bf16[1,2048,3072]{2,1,0:T(8,128)(2,1)} %param.11), kind=kOutput, calls=%fused_computation.6 | convolution fusion | flops 2717908992 | bytes 16121856 | tf_op jit(solution)/shard_map/tlcf,lfd->dtlc/dot_general | solution.py:57
  74.2 53.2 %reduce-scatter.2.cloned.1.call-done = f32[768,216]{0,1:T(8,128)} async-done(((f32[3072,216]{0,1:T(8,128)}), f32[768,216]{0,1:T(8,128)}) %reduce-scatter.2.cloned.1.call-update) | async-done | bytes 663568 | tf_op jit(solution)/shard_map/reduce_scatter | solution.py:58
  127.4 1.1 convert_bitcast_fusion
  128.5 0.1 all_to_all.16
  128.6 9.4 %all_to_all.22 = bf16[4,54,768]{2,1,0:T(8,128)(2,1)S(1)} all-to-all(bf16[4,54,768]{2,1,0:T(8,128)(2,1)S(1)} %all_to_all.16), channel_id=1, replica_groups=mesh['rep'=2,'tp'=4,'ep'=4] {'ep'}, dimensions={0} | all-to-all | bytes 663552 | tf_op jit(solution)/shard_map/all_to_all | solution.py:66
  138.0 0.1 all_to_all.18
  138.1 1.0 convolution_convert_fusion.1
  (10 shorter events, 0.2 us)
Async XLA Ops:
  6.5 120.8 %reduce-scatter.2.cloned.1.call-start = ((), (), s32[]{:S(2)}) async-start(), calls=%async_computation.3 | async-start | bytes 3317760 | tf_op jit(solution)/shard_map/reduce_scatter | solution.py:58
Sparse Core Ops, SparseCore 0:
  74.3 53.0 reduce-scatter.1
where the time goes:
time: 146 us
  waiting for transfers between devices  53.2 us (36%)
  blocking collectives  48.4 us (33%)
  matrix products  24.6 us (17%)
  between operations  13.5 us (9%)
  other arithmetic  4.01 us (3%)
  local copies, waits for them, and re-layouts  2.2 us (2%)
    reduce_scatter x1, waiting for transfers between devices, body(): lax.psum_scatter(part.reshape(columns // tp_count * lax.axis_size('tp'),...  53.2 us
    all_to_all x1, blocking collectives, body(): lax.all_to_all(packed, 'ep', split_axis=0, concat_axis=0, tiled=True)  20.5 us
    all_gather x1, blocking collectives, body(): whole = lax.all_gather(tokens, 'tp', axis=1, tiled=True)  18.5 us
    all_to_all x1, blocking collectives, body(): lax.all_to_all(expert_out, 'ep', split_axis=0, concat_axis=0, tiled=True)  9.41 us
    dot_general x1, matrix products, body(): jnp.einsum('tlcf,lfd->dtlc', hidden, expert_down, preferred_element_type=...  9.01 us
    dot_general x1, matrix products, hidden_rows(): jnp.einsum('tlcd,ldf->tlcf', row_block, expert_up, preferred_element_type...  7.89 us
    dot_general x1, matrix products, hidden_rows(): jnp.einsum('tlcd,ldf->tlcf', row_block, expert_gate, preferred_element_ty...  6.26 us
  transfers between devices with their start and end apart: 1, of which 1 were waited for; matrix products, arithmetic and copies ran while one was open for 0% of the time, Pallas kernels for 0%

commit v1 on v0

--- a/solution.py
+++ b/solution.py
@@ -2,6 +2,7 @@
 import jax.numpy as jnp
 from jax import lax
 from jax.sharding import PartitionSpec as P
+from jax.lax import axis_index, axis_size, ppermute
 
 
 def slot_tables(routing, route_gates, experts, capacity):
@@ -46,9 +47,32 @@
     experts = local_count * ep_count
     dispatch, combine = slot_tables(routing, route_gates, experts, capacity)
     dispatch_low = dispatch.astype(jnp.bfloat16)
-    whole = lax.all_gather(tokens, "tp", axis=1, tiled=True)
-    packed = jnp.einsum(
-        "tc,td->cd", dispatch_low, whole, preferred_element_type=jnp.float32
+
+    def _take_files(in_array, field):
+        lane_axis = "tp"
+        field_out, p_next, now = (axis_size(lane_axis), axis_index(lane_axis), in_array.shape[1])
+        u_next, newest = ([], [])
+        reply = all_rows = in_array
+        for h in range(field_out // 2 + 1):
+            u_next.append(field(reply, (p_next - h) % field_out * now))
+            if 0 < h < field_out - field_out // 2:
+                newest.append(field(all_rows, (p_next + h) % field_out * now))
+            column = []
+            for b in range(field_out):
+                column.append((b, (b + 1) % field_out))
+            reply = ppermute(reply, axis_name=lane_axis, perm=column)
+            tray = []
+            for b in range(field_out):
+                tray.append((b, (b - 1) % field_out))
+            all_rows = ppermute(all_rows, lane_axis, tray)
+        met_up = jnp.concatenate([*u_next[::-1], *newest], axis=1)
+        return jnp.roll(met_up, (p_next - field_out // 2) * u_next[0].shape[1], axis=1)
+
+    packed = _take_files(
+        tokens,
+        lambda part_2, start: jnp.einsum(
+            "tc,td->cd", dispatch_low, part_2, preferred_element_type=jnp.float32
+        ),
     ).astype(jnp.bfloat16)
     everyone = lax.all_to_all(packed, "ep", split_axis=0, concat_axis=0, tiled=True)
     total_rows = everyone.shape[0]

time: 146 us -> 141 us (0.966)
  blocking collectives: 48.4 us -> 30.1 us
  waiting for transfers between devices: 53.2 us -> 58.7 us
  starting transfers between devices: 0.01 us -> 5.08 us
  matrix products: 24.6 us -> 26.1 us
    all_gather x1 -> x0, blocking collectives: 18.5 us -> none  [body(): whole = lax.all_gather(tokens, 'tp', axis=1, tiled=True)]
    ppermute x0 -> x3, waiting for transfers between devices: none -> 7.59 us  [the longest x2 7.58 us: _take_files(): reply = ppermute(reply, axis_name=lane_axis, perm=column)]
    ppermute x0 -> x3, starting transfers between devices: none -> 5.08 us  [the longest x2 3.05 us: _take_files(): reply = ppermute(reply, axis_name=lane_axis, perm=column)]
    reduce_scatter x1, waiting for transfers between devices: 53.2 us -> 51.1 us  [body(): lax.psum_scatter(part.reshape(columns // tp_count * lax.axis_size('tp'),...]
    dot_general x1 -> x4, matrix products: 0.52 us -> 2 us  [body(): jnp.einsum('tc,td->cd', dispatch_low, part_2, preferred_element_type=jnp....]
  transfers between devices with their start and end apart: 1 -> 4, of which waited for: 1 -> 3; matrix products, arithmetic and copies ran while one was open for 0% -> 4% of each run, Pallas kernels for 0% -> 0%
where the time goes in v1:
time: 141 us; the launch traced here: 140 us
  waiting for transfers between devices  58.7 us (42%)
  blocking collectives  30.1 us (21%)
  matrix products  26.1 us (19%)
  between operations  13.5 us (10%)
  starting transfers between devices  5.08 us (4%)
  other arithmetic  3.98 us (3%)
  local copies, waits for them, and re-layouts  2.84 us (2%)
    reduce_scatter x1, waiting for transfers between devices, body(): lax.psum_scatter(part.reshape(columns // tp_count * lax.axis_size('tp'),...  51.1 us
    all_to_all x1, blocking collectives, body(): lax.all_to_all(packed, 'ep', split_axis=0, concat_axis=0, tiled=True)  20.7 us
    all_to_all x1, blocking collectives, body(): lax.all_to_all(expert_out, 'ep', split_axis=0, concat_axis=0, tiled=True)  9.41 us
    dot_general x1, matrix products, body(): jnp.einsum('tlcf,lfd->dtlc', hidden, expert_down, preferred_element_type=...  9.01 us
    dot_general x1, matrix products, hidden_rows(): jnp.einsum('tlcd,ldf->tlcf', row_block, expert_up, preferred_element_type...  7.89 us
    ppermute x2, waiting for transfers between devices, _take_files(): reply = ppermute(reply, axis_name=lane_axis, perm=column)  7.58 us
    dot_general x1, matrix products, hidden_rows(): jnp.einsum('tlcd,ldf->tlcf', row_block, expert_gate, preferred_element_ty...  6.25 us
    ppermute x2, starting transfers between devices, _take_files(): reply = ppermute(reply, axis_name=lane_axis, perm=column)  3.05 us
  transfers between devices with their start and end apart: 4, of which 3 were waited for; matrix products, arithmetic and copies ran while one was open for 4% of the time, Pallas kernels for 0%

profile of v1, /device:TPU:0, one launch (start us, length us, event | category | flops | bytes accessed | tf_op | source)
XLA Modules:
  0.0 140.3 jit_solution(15480073419589309196)
XLA Ops:
  6.5 3.1 %collective-permute-start = (bf16[96,768]{1,0:T(8,128)(2,1)}, bf16[96,768]{1,0:T(8,128)(2,1)S(1)}, u32[]{:S(2)}, u32[]{:S(2)}) collective-permute-start(bf16[96,768]{1,0:T(8,128)(2,1)} %param.6), channel_id=1, source_target_pairs={{0,4},{4,8},{8,12},{12,0},{1,5},{5,9},{9,13},{13,1},{2,6},{6,10},{... | collective-permute-start | bytes 442376 | tf_op jit(solution)/shard_map/ppermute | solution.py:63
  9.6 2.0 %collective-permute-start.2 = (bf16[96,768]{1,0:T(8,128)(2,1)}, bf16[96,768]{1,0:T(8,128)(2,1)S(1)}, u32[]{:S(2)}, u32[]{:S(2)}) collective-permute-start(bf16[96,768]{1,0:T(8,128)(2,1)} %param.6), channel_id=1, source_target_pairs={{0,12},{4,0},{8,4},{12,8},{1,13},{5,1},{9,5},{13,9},{2,14},{6,2},{... | collective-permute-start | bytes 442376 | tf_op jit(solution)/shard_map/ppermute | solution.py:67
  11.6 0.8 copy.23
  12.6 1.2 reduce-window.6
  14.2 0.1 reduce_sum.30
  14.4 2.1 %collective-permute-done = bf16[96,768]{1,0:T(8,128)(2,1)S(1)} collective-permute-done((bf16[96,768]{1,0:T(8,128)(2,1)}, bf16[96,768]{1,0:T(8,128)(2,1)S(1)}, u32[]{:S(2)}, u32[]{:S(2)}) %collective-permute-start) | collective-permute-done | bytes 147488 | tf_op jit(solution)/shard_map/ppermute | solution.py:63
  16.6 0.7 multiply_add_fusion
  17.3 0.8 convert_reduce_fusion
  18.1 5.4 %collective-permute-done.1 = bf16[96,768]{1,0:T(8,128)(2,1)S(1)} collective-permute-done((bf16[96,768]{1,0:T(8,128)(2,1)S(1)}, bf16[96,768]{1,0:T(8,128)(2,1)S(1)}, u32[]{:S(2)}, u32[]{:S(2)}) %collective-permute-start.1) | collective-permute-done | bytes 147488 | tf_op jit(solution)/shard_map/ppermute | solution.py:63
  23.5 0.3 constant_dynamic-update-slice_fusion.7
  23.8 0.3 constant_dynamic-update-slice_fusion.6
  24.1 1.2 constant_dynamic-update-slice_fusion.5
  25.3 0.3 constant_dynamic-update-slice_fusion.4
  25.7 0.5 dynamic-slice_convert_fusion
  26.2 0.4 all_to_all.14
  26.6 20.7 %all_to_all.21 = bf16[4,54,3072]{2,1,0:T(8,128)(2,1)S(1)} all-to-all(bf16[4,54,3072]{2,1,0:T(8,128)(2,1)S(1)} %all_to_all.14), channel_id=1, replica_groups=mesh['rep'=2,'tp'=4,'ep'=4] {'ep'}, dimensions={0} | all-to-all | bytes 2654208 | tf_op jit(solution)/shard_map/all_to_all | solution.py:77
  47.3 6.3 %fusion.9 = f32[4,1,54,2048]{3,2,0,1:T(8,128)S(1)} fusion(bf16[4,54,3072]{2,1,0:T(8,128)(2,1)S(1)} %all_to_all.21, bf16[1,3072,2048]{2,1,0:T(8,128)(2,1)} %param.9), kind=kOutput, calls=%fused_computation.7 | convolution fusion | flops 2717908992 | bytes 15679488 | tf_op jit(solution)/shard_map/tlcd,ldf->tlcf/dot_general | solution.py:34
  53.6 7.9 %fusion.18 = bf16[4,1,54,2048]{3,2,0,1:T(8,128)(2,1)S(1)} fusion(bf16[4,54,3072]{2,1,0:T(8,128)(2,1)S(1)} %all_to_all.21, bf16[1,3072,2048]{2,1,0:T(8,128)(2,1)} %param.10, f32[4,1,54,2048]{3,2,0,1:T(8,128)S(1)} %fusion.9), kind=kOutput, calls=%fused_computation.11 | convolution fusion | flops 2720563200 | bytes 16564224 | tf_op jit(solution)/shard_map/tlcd,ldf->tlcf/dot_general | solution.py:37
  61.5 0.2 dot_general.46
  61.7 9.0 %fusion.6 = f32[3072,216]{0,1:T(8,128)} fusion(bf16[216,2048]{1,0:T(8,128)(2,1)S(1)} %dot_general.46, bf16[1,2048,3072]{2,1,0:T(8,128)(2,1)} %param.11), kind=kOutput, calls=%fused_computation.6 | convolution fusion | flops 2717908992 | bytes 16121856 | tf_op jit(solution)/shard_map/tlcf,lfd->dtlc/dot_general | solution.py:81
  70.7 51.1 %reduce-scatter.2.cloned.1.call-done = f32[768,216]{0,1:T(8,128)} async-done(((f32[3072,216]{0,1:T(8,128)}), f32[768,216]{0,1:T(8,128)}) %reduce-scatter.2.cloned.1.call-update) | async-done | bytes 663568 | tf_op jit(solution)/shard_map/reduce_scatter | solution.py:82
  121.8 1.1 convert_bitcast_fusion
  123.0 9.4 %all_to_all.22 = bf16[4,54,768]{2,1,0:T(8,128)(2,1)S(1)} all-to-all(bf16[4,54,768]{2,1,0:T(8,128)(2,1)S(1)} %all_to_all.16), channel_id=1, replica_groups=mesh['rep'=2,'tp'=4,'ep'=4] {'ep'}, dimensions={0} | all-to-all | bytes 663552 | tf_op jit(solution)/shard_map/all_to_all | solution.py:90
  132.5 1.0 convolution_convert_fusion
  (23 shorter events, 1.0 us)
Async XLA Ops:
  6.5 115.3 %reduce-scatter.2.cloned.1.call-start = ((), (), s32[]{:S(2)}) async-start(), calls=%async_computation.3 | async-start | bytes 3317760 | tf_op jit(solution)/shard_map/reduce_scatter | solution.py:82
  6.5 10.0 %collective-permute-start = (bf16[96,768]{1,0:T(8,128)(2,1)}, bf16[96,768]{1,0:T(8,128)(2,1)S(1)}, u32[]{:S(2)}, u32[]{:S(2)}) collective-permute-start(bf16[96,768]{1,0:T(8,128)(2,1)} %param.6), channel_id=1, source_target_pairs={{0,4},{4,8},{8,12},{12,0},{1,5},{5,9},{9,13},{13,1},{2,6},{6,10},{... | collective-permute-start | bytes 442376 | tf_op jit(solution)/shard_map/ppermute | solution.py:63
  9.6 15.7 %collective-permute-start.2 = (bf16[96,768]{1,0:T(8,128)(2,1)}, bf16[96,768]{1,0:T(8,128)(2,1)S(1)}, u32[]{:S(2)}, u32[]{:S(2)}) collective-permute-start(bf16[96,768]{1,0:T(8,128)(2,1)} %param.6), channel_id=1, source_target_pairs={{0,12},{4,0},{8,4},{12,8},{1,13},{5,1},{9,5},{13,9},{2,14},{6,2},{... | collective-permute-start | bytes 442376 | tf_op jit(solution)/shard_map/ppermute | solution.py:67
  16.6 6.9 %collective-permute-start.1 = (bf16[96,768]{1,0:T(8,128)(2,1)S(1)}, bf16[96,768]{1,0:T(8,128)(2,1)S(1)}, u32[]{:S(2)}, u32[]{:S(2)}) collective-permute-start(bf16[96,768]{1,0:T(8,128)(2,1)S(1)} %collective-permute-done), channel_id=1, source_target_pairs={{0,4},{4,8},{8,12},{12,0},{1,5},{5,9},{9,13},{13,1},{2,6},{6,10},{... | collective-permute-start | bytes 442376 | tf_op jit(solution)/shard_map/ppermute | solution.py:63
Sparse Core Ops, SparseCore 0:
  70.9 50.9 reduce-scatter.1
